TPU v7x, 512 devices: a whole 4x8x8 slice. The times are simulated.
512 devices in a mesh: rows: 128 (over z, y, core), trees: 4 (over x).
Axes of the slice: x: 4, y: 8, z: 8, core: 2. Of those that a mesh axis runs over, the one named last changes fastest.
Arguments:
- node_of_row: int32 [4, 262144], P('trees', 'rows'), may hold values from 0 to 63
- bag_weight: int32 [4, 262144], P('trees', 'rows'), may hold values from 0 to 6, as said below
- smaller_side: int32 [4, 32], P('trees'), may hold values from 0 to 1
- bins: int32 [262144, 256], P('rows'), may hold values from 0 to 31
- target: float32 [262144], P('rows'), may hold values from -6 to 6
- parent_hist: float32 [4, 256, 3072], P('trees', 'rows')
Outputs:
- child_hist: float32 [4, 256, 6144], P('trees', 'rows')
- best_gain: float32 [4, 64], P('trees')
- importance: float32 [256], P('rows')
Inputs may be any that keep to these rules, and one draw needn't show every extreme that they name: `bag_weight`: poisson weights with mean one.
All inputs are finite; a program needn't handle non-finite values.
Results may differ from a plain program's by a relative error of at most 0.002.
Values sent between devices are 32-bit elements; how exact they have to be, the bound alone decides.
A program may use at most 64 MiB of HBM per device.

v0:
```python
import math

import jax
import jax.numpy as jnp
from jax import lax
from jax.sharding import Mesh
from jax.sharding import PartitionSpec as P

BINS = 32
ROWS = ("rows_0", "rows_1", "rows_2")


def cut_along(array, dim, peers):
    before, after = (array.shape[:dim], array.shape[dim + 1 :])
    return jnp.moveaxis(array.reshape(*before, peers, -1, *after), dim, 0)


def sum_at_owner(array, axis, dim):
    parts = cut_along(array, dim, lax.axis_size(axis))
    arrived = lax.all_to_all(parts, axis, split_axis=0, concat_axis=0, tiled=True)
    return arrived.sum(axis=0)


def summed_rows(array, axes, dim):
    far, near = axes
    parts = cut_along(array, dim, lax.axis_size(far))
    nearer = sum_at_owner(parts, near, dim + 1)
    arrived = lax.all_to_all(nearer, far, split_axis=0, concat_axis=0, tiled=True)
    return arrived.sum(axis=0)


def from_everyone(array, axis):
    copies = jnp.broadcast_to(array, (lax.axis_size(axis), *array.shape))
    return lax.all_to_all(copies, axis, split_axis=0, concat_axis=0, tiled=True)


def of_everyone(array, axis):
    return from_everyone(array, axis).max(axis=0)


def one_axis_at_a_time(array, axes):
    far, near = axes
    nearer = of_everyone(array, near)
    return of_everyone(nearer, far)


def taken_together(array, axis):
    return from_everyone(array, axis).sum(axis=0)


def shards(node_of_row, bag_weight, smaller_side, bins, target, parent_hist):
    nrows = bins.shape[0]
    feat = bins.shape[1]
    pairs = smaller_side.shape[1]
    nbins = BINS
    nodes = node_of_row[0]
    flags = smaller_side[0]
    pair = nodes // 2
    side = nodes % 2
    pair_hot = pair[:, None] == jnp.arange(pairs, dtype=jnp.int32)[None, :]
    flag_row = jnp.sum(jnp.where(pair_hot, flags[None, :], 0), axis=1)
    keep = (side == flag_row).astype(jnp.float32)
    wk = bag_weight[0].astype(jnp.float32) * keep
    stats = jnp.stack([wk, wk * target, wk * target * target], axis=1).astype(jnp.bfloat16)
    spread = (pair_hot.astype(jnp.bfloat16)[:, :, None] * stats[:, None, :]).reshape(
        nrows, pairs * 3
    )
    levels = jnp.arange(nbins, dtype=jnp.int32)
    owned = feat // lax.axis_size(ROWS)
    width = math.gcd(owned * lax.axis_size(ROWS), 32)

    def one_block(index):
        cols = lax.dynamic_slice_in_dim(bins, index * width, width, 1)
        onehot = (
            (cols[:, :, None] == levels[None, None, :])
            .astype(jnp.bfloat16)
            .reshape(nrows, width * nbins)
        )
        part = jnp.einsum("rk,rm->km", onehot, spread, preferred_element_type=jnp.float32)
        return part.reshape(width, nbins * pairs * 3)

    blocks = lax.map(one_block, jnp.arange(owned * lax.axis_size(ROWS) // width, dtype=jnp.int32))
    small = summed_rows(
        blocks.reshape(owned * lax.axis_size(ROWS), nbins * pairs * 3),
        (("rows_0", "rows_1"), "rows_2"),
        0,
    )
    small = small.reshape(owned, nbins, pairs, 3)
    parent = parent_hist[0].reshape(owned, nbins, pairs, 3)
    sibling = parent - small
    take = jnp.arange(2, dtype=jnp.int32)[None, :] == flags[:, None]
    children = jnp.where(
        take[None, None, :, :, None], small[:, :, :, None, :], sibling[:, :, :, None, :]
    )
    children = children.reshape(owned, nbins, 2 * pairs, 3)
    count = children[..., 0]
    total = children[..., 1]
    ccum = jnp.cumsum(count, axis=1)
    scum = jnp.cumsum(total, axis=1)
    call = ccum[:, -1:, :]
    sall = scum[:, -1:, :]
    left_c = ccum[:, :-1, :]
    left_s = scum[:, :-1, :]
    gain = left_s * left_s / (jnp.maximum(left_c, 0.0) + 1.0)
    gain = gain + (sall - left_s) ** 2 / (jnp.maximum(call - left_c, 0.0) + 1.0)
    gain = gain - sall * sall / (jnp.maximum(call, 0.0) + 1.0)
    fgain = jnp.max(gain, axis=1)
    best = one_axis_at_a_time(jnp.max(fgain, axis=0), (("rows_0", "rows_1"), "rows_2"))
    featsum = taken_together(jnp.sum(fgain, axis=1), "trees")
    importance = featsum / (lax.axis_size("trees") * node_of_row.shape[0] * 2 * pairs)
    child_hist = children.reshape(owned, nbins * 2 * pairs * 3)
    return (child_hist[None], best[None], importance)


def solution(mesh):
    finer = Mesh(
        mesh.devices.reshape(8, 8, 2, mesh.shape["trees"]), ("rows_0", "rows_1", "rows_2", "trees")
    )
    return jax.shard_map(
        shards,
        mesh=finer,
        in_specs=(
            P("trees", ROWS),
            P("trees", ROWS),
            P("trees", None),
            P(ROWS, None),
            P(ROWS),
            P("trees", ROWS, None),
        ),
        out_specs=(P("trees", ROWS, None), P("trees", None), P(ROWS)),
        check_vma=False,
    )
```

profile of v0, /device:TPU:1, one launch (start us, length us, event | category | flops | bytes accessed | tf_op | source)
XLA Modules:
  0.0 181.2 jit_solution(6007261283232035666)
XLA Ops:
  5.1 2.9 %copy.47 = s32[2048,256]{0,1:T(8,128)} copy(s32[2048,256]{1,0:T(8,128)} %param.11) | data formatting | bytes 4194304
  8.1 54.0 %while.11 = (s32[]{:T(128)}, f32[8,32,3072]{2,1,0:T(8,128)}, s32[8]{0:T(128)S(1)}, s32[2048,256]{0,1:T(8,128)}, bf16[2048,3]{0,1:T(4,128)(2,1)S(1)}, /*index=5*/...) while((s32[]{:T(128)}, f32[8,32,3072]{2,1,0:T(8,128)}, ...), condition=%wide.region_2.3_spmd.clone, body=%wide.region_1.2_spmd.clone.sunk | while | flops 404946944 | bytes 8680099 | solution.py:82
  10.4 1.5 bitcast_compare_fusion.2
  17.1 1.5 bitcast_compare_fusion.2
  23.8 1.5 bitcast_compare_fusion.2
  30.6 1.5 bitcast_compare_fusion.2
  37.3 1.5 bitcast_compare_fusion.2
  44.1 1.5 bitcast_compare_fusion.2
  50.8 1.5 bitcast_compare_fusion.2
  57.6 1.5 bitcast_compare_fusion.2
  59.7 1.2 fusion.21
  62.0 3.7 %reshape_reshape_reshape.3 = f32[64,2,2,3072]{3,2,1,0:T(2,128)S(1)} reshape(f32[8,32,3072]{2,1,0:T(8,128)} %get-tuple-element.35) | data formatting | bytes 6291456 | tf_op jit(solution)/shard_map/reshape;reshape;reshape | solution.py:15
  66.0 12.7 %all_to_all.28 = f32[2,64,2,3072]{3,2,1,0:T(2,128)S(1)} all-to-all(f32[2,64,2,3072]{3,2,1,0:T(2,128)S(1)} %copy.48), channel_id=1, replica_groups=mesh['rows_0'=8,'rows_1'=8,'rows_2'=2,'trees'=4] {'rows_2'}, dimensions={0} | all-to-all | bytes 6291456 | tf_op jit(solution)/shard_map/all_to_all | solution.py:20
  78.7 3.8 %reduce_sum.49 = f32[64,2,3072]{2,1,0:T(2,128)} reduce(f32[2,64,2,3072]{3,2,1,0:T(2,128)S(1)} %all_to_all.28, f32[]{:T(128)} %constant.53.clone.1), dimensions={0}, to_apply=%region_3.4 | reduce | flops 393216 | bytes 4718596 | tf_op jit(solution)/shard_map/reduce_sum | solution.py:21
  82.5 11.3 %all-to-all-start.1 = ((f32[64,2,3072]{2,1,0:T(2,128)}), f32[64,2,3072]{2,1,0:T(2,128)S(1)}, u32[]{:S(2)}, u32[]{:S(2)}) async-start(f32[64,2,3072]{2,1,0:T(2,128)} %reduce_sum.49), calls=%async_computation.1 | async-start | bytes 3145728 | tf_op jit(solution)/shard_map/all_to_all | solution.py:28
  96.4 36.6 %all-to-all-done.1 = f32[64,2,3072]{2,1,0:T(2,128)S(1)} async-done(((f32[64,2,3072]{2,1,0:T(2,128)}), f32[64,2,3072]{2,1,0:T(2,128)S(1)}, u32[]{:S(2)}, u32[]{:S(2)}) %all-to-all-start.1) | async-done | bytes 1572896 | tf_op jit(solution)/shard_map/all_to_all | solution.py:28
  137.1 6.1 %all-to-all-start.2 = ((f32[2,1,64]{2,1,0:T(1,128)}), f32[2,1,64]{2,1,0:T(1,128)S(1)}, u32[]{:S(2)}, u32[]{:S(2)}) async-start(f32[2,1,64]{2,1,0:T(1,128)} %broadcast_in_dim.94), calls=%async_computation.2 | async-start | bytes 2048 | tf_op jit(solution)/shard_map/all_to_all | solution.py:34
  143.3 2.1 %broadcast_in_dim.89.clone = f32[2,32,32,2,3]{4,3,2,1,0:T(2,128)} broadcast(f32[2,32,32,3]{3,2,1,0:T(8,128)S(1)} %sub.44), dimensions={0,1,2,4} | broadcast | bytes 73728 | tf_op jit(solution)/shard_map/jit(_where)/broadcast_in_dim | solution.py:92
  145.4 4.3 %broadcast_in_dim.90 = f32[1,2,6144]{2,1,0:T(2,128)S(1)} reshape(f32[2,32,32,2,3]{4,3,2,1,0:T(2,128)} %broadcast_in_dim.89.clone) | data formatting | bytes 98304 | tf_op jit(solution)/shard_map/jit(_where)/broadcast_in_dim | solution.py:92
  150.5 2.7 %broadcast_in_dim.88 = f32[1,2,6144]{2,1,0:T(2,128)S(1)} reshape(f32[2,32,32,2,3]{4,3,2,1,0:T(2,128)S(1)} %broadcast_in_dim.87.clone) | data formatting | bytes 98304 | tf_op jit(solution)/shard_map/jit(_where)/broadcast_in_dim | solution.py:92
  153.8 4.0 %all-to-all-start.4 = ((f32[4,1,2]{2,1,0:T(1,128)}), f32[4,1,2]{2,1,0:T(1,128)S(1)}, u32[]{:S(2)}, u32[]{:S(2)}) async-start(f32[4,1,2]{2,1,0:T(1,128)} %broadcast_in_dim.97), calls=%async_computation.4 | async-start | bytes 4096 | tf_op jit(solution)/shard_map/all_to_all | solution.py:34
  158.5 3.5 %all-to-all-done.4 = f32[4,1,2]{2,1,0:T(1,128)S(1)} async-done(((f32[4,1,2]{2,1,0:T(1,128)}), f32[4,1,2]{2,1,0:T(1,128)S(1)}, u32[]{:S(2)}, u32[]{:S(2)}) %all-to-all-start.4) | async-done | bytes 64 | tf_op jit(solution)/shard_map/all_to_all | solution.py:34
  162.6 7.3 %all-to-all-start.3 = ((f32[64,1,64]{2,1,0:T(1,128)}), f32[64,1,64]{2,1,0:T(1,128)S(1)}, u32[]{:S(2)}, u32[]{:S(2)}) async-start(f32[64,1,64]{2,1,0:T(1,128)} %broadcast_in_dim.95), calls=%async_computation.3 | async-start | bytes 65536 | tf_op jit(solution)/shard_map/all_to_all | solution.py:34
  170.4 10.3 %all-to-all-done.3 = f32[64,1,64]{2,1,0:T(1,128)S(1)} async-done(((f32[64,1,64]{2,1,0:T(1,128)}), f32[64,1,64]{2,1,0:T(1,128)S(1)}, u32[]{:S(2)}, u32[]{:S(2)}) %all-to-all-start.3) | async-done | bytes 16416 | tf_op jit(solution)/shard_map/all_to_all | solution.py:34
  (119 shorter events, 50.1 us)
Async XLA Ops:
  82.5 11.3 %copy-start = (f32[1,2,3072]{2,1,0:T(2,128)S(1)}, f32[1,2,3072]{2,1,0:T(2,128)}, u32[]{:S(2)}) copy-start(f32[1,2,3072]{2,1,0:T(2,128)} %param.13) | copy-start | bytes 73732
  82.5 12.2 %copy-start.1 = (s32[1,32]{1,0:T(1,128)S(1)}, s32[1,32]{1,0:T(1,128)}, u32[]{:S(2)}) copy-start(s32[1,32]{1,0:T(1,128)} %param.10) | copy-start | bytes 388
  82.5 50.5 %all-to-all-start.1 = ((f32[64,2,3072]{2,1,0:T(2,128)}), f32[64,2,3072]{2,1,0:T(2,128)S(1)}, u32[]{:S(2)}, u32[]{:S(2)}) async-start(f32[64,2,3072]{2,1,0:T(2,128)} %reduce_sum.49), calls=%async_computation.1 | async-start | bytes 3145728 | tf_op jit(solution)/shard_map/all_to_all | solution.py:28
  137.1 16.1 %all-to-all-start.2 = ((f32[2,1,64]{2,1,0:T(1,128)}), f32[2,1,64]{2,1,0:T(1,128)S(1)}, u32[]{:S(2)}, u32[]{:S(2)}) async-start(f32[2,1,64]{2,1,0:T(1,128)} %broadcast_in_dim.94), calls=%async_computation.2 | async-start | bytes 2048 | tf_op jit(solution)/shard_map/all_to_all | solution.py:34
  153.8 8.2 %all-to-all-start.4 = ((f32[4,1,2]{2,1,0:T(1,128)}), f32[4,1,2]{2,1,0:T(1,128)S(1)}, u32[]{:S(2)}, u32[]{:S(2)}) async-start(f32[4,1,2]{2,1,0:T(1,128)} %broadcast_in_dim.97), calls=%async_computation.4 | async-start | bytes 4096 | tf_op jit(solution)/shard_map/all_to_all | solution.py:34
  162.6 18.1 %all-to-all-start.3 = ((f32[64,1,64]{2,1,0:T(1,128)}), f32[64,1,64]{2,1,0:T(1,128)S(1)}, u32[]{:S(2)}, u32[]{:S(2)}) async-start(f32[64,1,64]{2,1,0:T(1,128)} %broadcast_in_dim.95), calls=%async_computation.3 | async-start | bytes 65536 | tf_op jit(solution)/shard_map/all_to_all | solution.py:34
where the time goes:
time: 183 us; the launch traced here: 181 us
  waiting for transfers between devices  50.4 us (28%)
  local copies, waits for them, and re-layouts  47.6 us (26%)
  starting transfers between devices  28.6 us (16%)
  other arithmetic  25.5 us (14%)
  blocking collectives  12.7 us (7%)
  matrix products  9.93 us (5%)
  loops' own time  5.57 us (3%)
    all_to_all x1, waiting for transfers between devices, summed_rows(): lax.all_to_all(nearer, far, split_axis=0, concat_axis=0, tiled=True)  36.6 us
    all_to_all x3, starting transfers between devices, from_everyone(): return lax.all_to_all(copies, axis, split_axis=0, concat_axis=0, tiled=True)  17.4 us
    all_to_all x3, waiting for transfers between devices, from_everyone(): return lax.all_to_all(copies, axis, split_axis=0, concat_axis=0, tiled=True)  13.8 us
    broadcast_in_dim x10, local copies, waits for them, and re-layouts, shards(): jnp.where(take[None, None, :, :, None], small[:, :, :, None, :], sibling[...  12.9 us
    all_to_all x1, blocking collectives, sum_at_owner(): lax.all_to_all(parts, axis, split_axis=0, concat_axis=0, tiled=True)  12.7 us
    eq x8, other arithmetic, one_block(): cols[:, :, None] == levels[None, None, :]  12.1 us
    all_to_all x1, starting transfers between devices, summed_rows(): lax.all_to_all(nearer, far, split_axis=0, concat_axis=0, tiled=True)  11.3 us
    dot_general x8, matrix products, one_block(): jnp.einsum('rk,rm->km', onehot, spread, preferred_element_type=jnp.float32)  9.93 us
  transfers between devices with their start and end apart: 4, of which 3 were waited for; matrix products, arithmetic and copies ran while one was open for 8% of the time, Pallas kernels for 0%

commit v1 on v0

v1 whole, which is shorter than its diff:
```python
import functools

import jax
import jax.numpy as jnp
from jax import lax
from jax.experimental import pallas as pl
from jax.experimental.pallas import tpu as pltpu
from jax.sharding import Mesh
from jax.sharding import PartitionSpec as P

ROWS = ("rows_0", "rows_1", "rows_2")
MESH = pl.DeviceIdType.MESH
HIGHEST = lax.Precision.HIGHEST
f32 = jnp.float32
bf16 = jnp.bfloat16
i32 = jnp.int32

ORDER = (4, 3, -3, 2, -2, 1, -1, 0)
SLOT = {delta: i for i, delta in enumerate(ORDER)}
NR = 2048
LOW = -3.0e38


def iota(shape, dim):
    return lax.broadcasted_iota(i32, shape, dim)


def kernel(
    node_h, bag_h, flag_h, bins_h, tgt_h, par_h,
    child_o, best_o, imp_o,
    node_v, bag_v, flag_v, bins_v, tgt_v, par_v,
    bins_b, ev, spread, own, peer, core_r, ring_r, turned, quad_r,
    p16, pchild, amat,
    best_s, best_ra, best_t, best_rb, imp_s, imp_r,
    in_sem, core_ss, core_rs, ring_ss, ring_rs, quad_ss, quad_rs,
    ba_ss, ba_rs, bb_ss, bb_rs, im_ss, im_rs,
):
    z = lax.axis_index("rows_0")
    y = lax.axis_index("rows_1")
    c = lax.axis_index("rows_2")
    t = lax.axis_index("trees")

    def wrap(v, n):
        return lax.rem(v + n, n)

    def along_y(off, oc=0):
        return (z, lax.rem(y + off, 8), lax.rem(c + oc, 2), t)

    def along_z(off):
        return (lax.rem(z + off, 8), y, c, t)

    def along_x(off):
        return (z, y, c, lax.rem(t + off, 4))

    def along_p(off):
        off = off % 8
        return (lax.rem(z + off * c, 8), lax.rem(y + off * (1 - c), 8), c, t)

    def along_q(off):
        return (lax.rem(z + off * (1 - c), 8), lax.rem(y + off * c, 8), c, t)

    loads = []
    for i in range(8):
        cp = pltpu.make_async_copy(
            bins_h.at[pl.ds(256 * i, 256)], bins_v.at[pl.ds(256 * i, 256)], in_sem.at[i]
        )
        cp.start()
        loads.append(cp)
    small = []
    for i, (src, dst) in enumerate(
        ((node_h, node_v), (bag_h, bag_v), (flag_h, flag_v), (tgt_h, tgt_v), (par_h, par_v))
    ):
        cp = pltpu.make_async_copy(src, dst, in_sem.at[8 + i])
        cp.start()
        small.append(cp)

    barrier = pltpu.get_barrier_semaphore()
    greeted = 0
    for oy in range(8):
        for oc in range(2):
            if oy or oc:
                pl.semaphore_signal(barrier, inc=1, device_id=along_y(oy, oc), device_id_type=MESH)
                greeted += 1
    for off in range(1, 8):
        pl.semaphore_signal(barrier, inc=1, device_id=along_z(off), device_id_type=MESH)
        greeted += 1
    for off in range(1, 4):
        pl.semaphore_signal(barrier, inc=1, device_id=along_x(off), device_id_type=MESH)
        greeted += 1

    for cp in small:
        cp.wait()
    flags = flag_v[...]
    row96 = iota((96, 1), 0)
    pair96 = lax.div(row96, 3)
    stat96 = row96 - 3 * pair96
    flag96 = jnp.sum(
        jnp.where(iota((96, 32), 1) == lax.div(iota((96, 32), 0), 3), flags, 0), axis=1, keepdims=True
    )
    chosen = 2 * pair96 + flag96
    for i in range(4):
        part = pl.ds(512 * i, 512)
        node = node_v[:, part]
        wk = bag_v[:, part].astype(f32)
        tgt = tgt_v[:, part]
        first = wk * tgt
        second = first * tgt
        stat = jnp.where(stat96 == 0, wk, jnp.where(stat96 == 1, first, second))
        spread[:, part] = jnp.where(node == chosen, stat, 0.0).astype(bf16)

    for i in range(8):
        loads[i].wait()
        part = pl.ds(256 * i, 256)
        bins_b[part, :] = bins_v[part, :].astype(bf16)

    lane256 = iota((1, 256), 1)
    lane_dd = lax.div(lane256, 128)
    lane_q = lax.rem(lax.div(lane256, 16), 8)
    lane_k = lax.rem(lax.div(lane256, 8), 2)
    lane_b = (4 * lax.rem(lane256, 8)).astype(f32)

    def tile(pair_i, h, dst):
        pos = y * (1 - h) + z * h
        d0 = wrap(pos + ORDER[2 * pair_i], 8)
        d1 = wrap(pos + ORDER[2 * pair_i + 1], 8)
        d = d0 + (d1 - d0) * lane_dd
        source = lane_q * (32 - 28 * h) + d * (4 + 28 * h) + 2 * h + lane_k
        expand = jnp.where(iota((256, 256), 0) == source, 1.0, 0.0).astype(bf16)

        def widen(i, carry):
            part = pl.ds(pl.multiple_of(512 * i, 512), 512)
            ev[part, :] = jnp.dot(bins_b[part, :], expand, preferred_element_type=f32).astype(bf16)
            return carry

        lax.fori_loop(0, 4, widen, 0)

        def one(bh, carry):
            level = (lane_b + bh.astype(f32)).astype(bf16)
            acc = None
            for i in range(8):
                part = slice(256 * i, 256 * i + 256)
                hot = jnp.where(ev[part, :] == level, jnp.ones((), bf16), jnp.zeros((), bf16))
                term = jnp.dot(spread[:, part], hot, preferred_element_type=f32)
                acc = term if acc is None else acc + term
            at = pl.ds(pl.multiple_of(96 * bh, 96), 96)
            dst[2 * pair_i, at, :] = acc[:, :128]
            dst[2 * pair_i + 1, at, :] = acc[:, 128:]
            return carry

        lax.fori_loop(0, 4, one, 0)

    def core_copy(slot):
        return pltpu.make_async_remote_copy(
            src_ref=peer.at[slot], dst_ref=core_r.at[slot],
            send_sem=core_ss.at[slot], recv_sem=core_rs.at[slot],
            device_id=(z, y, 1 - c, t), device_id_type=MESH,
        )

    def ring_copy(way, step, half):
        delta = (4 - step) * (1 if way == 0 else -1)
        slot = SLOT[4 if step == 0 else delta]
        rows = pl.ds(192 * half, 192)
        return pltpu.make_async_remote_copy(
            src_ref=own.at[slot, rows], dst_ref=ring_r.at[way, step, rows],
            send_sem=ring_ss.at[way, step, half], recv_sem=ring_rs.at[way, step, half],
            device_id=along_p(1 if way == 0 else -1), device_id_type=MESH,
        )

    def halves(way, step):
        return (way,) if step == 0 else (0, 1)

    def merge_core(slot):
        core_copy(slot).wait_recv()
        own[slot] += core_r[slot]

    def step_sends(step):
        for half in (0, 1):
            for way in (0, 1):
                delta = (4 - step) * (1 if way == 0 else -1)
                slot = SLOT[delta]
                rows = pl.ds(192 * half, 192)
                if half in halves(way, step - 1):
                    ring_copy(way, step - 1, half).wait_recv()
                    own[slot, rows, :] += ring_r[way, step - 1, rows, :]
                ring_copy(way, step, half).start()

    for pair_i in range(4):
        tile(pair_i, 1 - c, peer)
        if pair_i == 0:
            pl.semaphore_wait(barrier, greeted)
        core_copy(2 * pair_i).start()
        core_copy(2 * pair_i + 1).start()
        tile(pair_i, c, own)
        merge_core(2 * pair_i)
        merge_core(2 * pair_i + 1)
        if pair_i == 0:
            ring_copy(0, 0, 0).start()
            ring_copy(1, 0, 1).start()
        else:
            step_sends(pair_i)

    flag384 = jnp.concatenate([flag96] * 4, axis=0)
    out_lane = iota((1, 768), 1)
    out_bh = lax.div(out_lane, 192)
    out_rest = out_lane - 192 * out_bh
    out_pair = lax.div(out_rest, 6)
    out_six = out_rest - 6 * out_pair
    out_child = lax.div(out_six, 3)
    out_from = 96 * out_bh + 3 * out_pair + (out_six - 3 * out_child)
    for k in range(2):
        for bl in range(8):
            p16[8 * k + bl : 8 * k + bl + 1, :] = par_v[0, k : k + 1, 384 * bl : 384 * bl + 384]
    match = iota((384, 768), 0) == out_from
    is_small = flag384 == out_child
    amat[...] = jnp.where(match, jnp.where(is_small, 1.0, -1.0), 0.0)
    bmat = jnp.where(match, jnp.where(is_small, 0.0, 1.0), 0.0)
    parent = p16[...]
    pchild[...] = jnp.dot(parent, bmat, preferred_element_type=f32, precision=HIGHEST)

    lane = iota((16, 384), 1)
    sub = lax.rem(iota((16, 384), 0), 8)

    def cumulative(x):
        x1 = x + jnp.where(lane >= 96, pltpu.roll(x, 96, 1), 0.0)
        x2 = x1 + jnp.where(lane >= 192, pltpu.roll(x1, 192, 1), 0.0)
        t3 = jnp.where(lane >= 288, x2, 0.0)
        t4 = t3 + pltpu.roll(t3, 96, 1)
        tot = t4 + pltpu.roll(t4, 192, 1)
        before = jnp.where(sub >= 1, pltpu.roll(tot, 1, 0), 0.0)
        for s in (1, 2, 4):
            before = before + jnp.where(sub >= s, pltpu.roll(before, s, 0), 0.0)
        whole = jnp.sum(tot.reshape(2, 8, 384), axis=1, keepdims=True)
        whole = jnp.broadcast_to(whole, (2, 8, 384)).reshape(16, 384)
        return x2 + before, whole

    def gain_of(cb, sb, call, sall):
        gain = sb * sb / (jnp.maximum(cb, 0.0) + 1.0)
        rest = sall - sb
        gain = gain + rest * rest / (jnp.maximum(call - cb, 0.0) + 1.0)
        gain = gain - sall * sall / (jnp.maximum(call, 0.0) + 1.0)
        gain = jnp.where((sub == 7) & (lane >= 288), LOW, gain)
        top = jnp.max(gain.reshape(2, 8, 384), axis=1, keepdims=True)
        top = jnp.broadcast_to(top, (2, 8, 384)).reshape(16, 384)
        top = jnp.maximum(top, pltpu.roll(top, 192, 1))
        return jnp.maximum(top, pltpu.roll(top, 96, 1))

    def left_one(x):
        return pltpu.roll(x, 383, 1)

    pcum, pall = cumulative(parent)
    psum, psall = left_one(pcum), left_one(pall)

    last = SLOT[0]
    total = own[last]
    for half in (0, 1):
        for way in (0, 1):
            ring_copy(way, 3, half).wait_recv()
    total = total + ring_r[0, 3] + ring_r[1, 3]
    turned[...] = total.T

    qpos = z * (1 - c) + y * c

    def quad_copy(off):
        to = lax.rem(qpos + off, 8)
        return pltpu.make_async_remote_copy(
            src_ref=turned.at[pl.ds(pl.multiple_of(16 * to, 16), 16)], dst_ref=quad_r.at[off],
            send_sem=quad_ss.at[off], recv_sem=quad_rs.at[off],
            device_id=along_q(off), device_id_type=MESH,
        )

    far_first = (4, 3, 5, 2, 6, 1, 7)
    for off in far_first:
        quad_copy(off).start()
    hist = turned[pl.ds(pl.multiple_of(16 * qpos, 16), 16), :]
    for off in (1, 7, 2, 6, 3, 5, 4):
        quad_copy(off).wait_recv()
        hist = hist + quad_r[off]

    scum, sall = cumulative(hist)
    ssum, ssall = left_one(scum), left_one(sall)
    gain_s = gain_of(scum, ssum, sall, ssall)
    gain_b = gain_of(pcum - scum, psum - ssum, pall - sall, psall - ssall)
    third = lax.rem(lane, 3)
    both = jnp.where((lane < 96) & (third == 0), gain_s + gain_b, 0.0)
    feat = jnp.sum(both, axis=1, keepdims=True)
    lane8 = iota((8, 128), 1)
    imp_s[...] = jnp.where(lane8 == 0, feat[0:8], jnp.where(lane8 == 1, feat[8:16], 0.0))
    top_s = jnp.maximum(gain_s[0:8], gain_s[8:16])
    top_b = jnp.maximum(gain_b[0:8], gain_b[8:16])
    mixed = jnp.where(third[0:8] == 0, top_s, pltpu.roll(top_b, 1, 1))
    best_s[...] = mixed[:, :128]

    def best_a(oy, oc):
        slot = 2 * oy + oc
        return pltpu.make_async_remote_copy(
            src_ref=best_s, dst_ref=best_ra.at[slot],
            send_sem=ba_ss.at[slot], recv_sem=ba_rs.at[slot],
            device_id=along_y(oy, oc), device_id_type=MESH,
        )

    def best_b(off):
        return pltpu.make_async_remote_copy(
            src_ref=best_t, dst_ref=best_rb.at[off],
            send_sem=bb_ss.at[off], recv_sem=bb_rs.at[off],
            device_id=along_z(off), device_id_type=MESH,
        )

    def imp_copy(off):
        return pltpu.make_async_remote_copy(
            src_ref=imp_s, dst_ref=imp_r.at[off],
            send_sem=im_ss.at[off], recv_sem=im_rs.at[off],
            device_id=along_x(off), device_id_type=MESH,
        )

    others = [(oy, oc) for oy in (4, 3, 5, 2, 6, 1, 7, 0) for oc in (0, 1) if oy or oc]
    for oy, oc in others:
        best_a(oy, oc).start()
    for off in (2, 1, 3):
        imp_copy(off).start()

    kids = pchild[...] + jnp.dot(hist, amat[...], preferred_element_type=f32, precision=HIGHEST)
    for k in range(2):
        for bl in range(8):
            child_o[0, k : k + 1, 768 * bl : 768 * bl + 768] = kids[8 * k + bl : 8 * k + bl + 1, :]

    top = best_s[...]
    for oy, oc in others:
        best_a(oy, oc).wait_recv()
        top = jnp.maximum(top, best_ra[2 * oy + oc])
    best_t[...] = top
    for off in far_first:
        best_b(off).start()

    flag_col = jnp.sum(jnp.where(iota((32, 32), 0) == iota((32, 32), 1), flags, 0), axis=1, keepdims=True)
    node_lane = iota((32, 64), 1)
    node_flag = jnp.sum(
        jnp.where(lax.div(node_lane, 2) == iota((32, 64), 0), flag_col, 0), axis=0, keepdims=True
    )
    q_lane = iota((1, 64), 1)
    q_pair = lax.div(q_lane, 2)
    taken = 3 * q_pair + jnp.where(q_lane - 2 * q_pair == node_flag, 0, 1)
    pick = jnp.where(iota((128, 64), 0) == taken, 1.0, 0.0)

    share = imp_s[...]
    for off in (1, 3, 2):
        imp_copy(off).wait_recv()
        share = share + imp_r[off]
    imp_o[...] = share[0:1, 0:2] * (1.0 / 256.0)

    for off in far_first:
        best_b(off).wait_recv()
        top = jnp.maximum(top, best_rb[off])
    best_o[...] = jnp.dot(top, pick, preferred_element_type=f32, precision=HIGHEST)[0:1, :]

    for slot in range(8):
        core_copy(slot).wait_send()
    for way in (0, 1):
        for step in range(4):
            for half in halves(way, step):
                ring_copy(way, step, half).wait_send()
    for off in range(1, 8):
        quad_copy(off).wait_send()
        best_b(off).wait_send()
    for oy, oc in others:
        best_a(oy, oc).wait_send()
    for off in range(1, 4):
        imp_copy(off).wait_send()


def shards(node_of_row, bag_weight, smaller_side, bins, target, parent_hist):
    any_space = pl.BlockSpec(memory_space=pl.ANY)
    vmem = pl.BlockSpec(memory_space=pltpu.VMEM)
    dma = pltpu.SemaphoreType.DMA
    child, best, imp = pl.pallas_call(
        kernel,
        out_shape=(
            jax.ShapeDtypeStruct((1, 2, 6144), f32),
            jax.ShapeDtypeStruct((1, 64), f32),
            jax.ShapeDtypeStruct((1, 2), f32),
        ),
        in_specs=[any_space] * 6,
        out_specs=(vmem, vmem, vmem),
        scratch_shapes=[
            pltpu.VMEM((1, NR), i32),
            pltpu.VMEM((1, NR), i32),
            pltpu.VMEM((1, 32), i32),
            pltpu.VMEM((NR, 256), i32),
            pltpu.VMEM((1, NR), f32),
            pltpu.VMEM((1, 2, 3072), f32),
            pltpu.VMEM((NR, 256), bf16),
            pltpu.VMEM((NR, 256), bf16),
            pltpu.VMEM((96, NR), bf16),
            pltpu.VMEM((8, 384, 128), f32),
            pltpu.VMEM((8, 384, 128), f32),
            pltpu.VMEM((8, 384, 128), f32),
            pltpu.VMEM((2, 4, 384, 128), f32),
            pltpu.VMEM((128, 384), f32),
            pltpu.VMEM((8, 16, 384), f32),
            pltpu.VMEM((16, 384), f32),
            pltpu.VMEM((16, 768), f32),
            pltpu.VMEM((384, 768), f32),
            pltpu.VMEM((8, 128), f32),
            pltpu.VMEM((16, 8, 128), f32),
            pltpu.VMEM((8, 128), f32),
            pltpu.VMEM((8, 8, 128), f32),
            pltpu.VMEM((8, 128), f32),
            pltpu.VMEM((4, 8, 128), f32),
            dma((13,)),
            dma((8,)), dma((8,)),
            dma((2, 4, 2)), dma((2, 4, 2)),
            dma((8,)), dma((8,)),
            dma((16,)), dma((16,)),
            dma((8,)), dma((8,)),
            dma((4,)), dma((4,)),
        ],
        compiler_params=pltpu.CompilerParams(
            collective_id=0, has_side_effects=True, vmem_limit_bytes=40 * 1024 * 1024
        ),
    )(node_of_row, bag_weight, smaller_side, bins, target.reshape(1, NR), parent_hist)
    return child, best, imp.reshape(2)


def solution(mesh):
    finer = Mesh(
        mesh.devices.reshape(8, 8, 2, mesh.shape["trees"]), ("rows_0", "rows_1", "rows_2", "trees")
    )
    return jax.shard_map(
        shards,
        mesh=finer,
        in_specs=(
            P("trees", ROWS),
            P("trees", ROWS),
            P("trees", None),
            P(ROWS, None),
            P(ROWS),
            P("trees", ROWS, None),
        ),
        out_specs=(P("trees", ROWS, None), P("trees", None), P(ROWS)),
        check_vma=False,
    )
```

time: 183 us -> 61.3 us (0.33)
  Pallas kernels: 0 us -> 53.6 us
  waiting for transfers between devices: 50.4 us -> 0 us
  local copies, waits for them, and re-layouts: 47.6 us -> 6.71 us
  starting transfers between devices: 28.6 us -> 0 us
  other arithmetic: 25.5 us -> 0 us
  blocking collectives: 12.7 us -> 0 us
  matrix products: 9.93 us -> 0 us
  loops' own time: 5.57 us -> 0 us
    pallas_call x0 -> x1, Pallas kernels: none -> 53.6 us  [shards(): pl.pallas_call(kernel, out_shape=(jax.ShapeDtypeStruct((1, 2, 6144), f32)...]
    all_to_all x4 -> x0, waiting for transfers between devices: 50.4 us -> none  [the longest x1 36.6 us: summed_rows(): lax.all_to_all(nearer, far, split_axis=0, concat_axis=0, tiled=True)]
    all_to_all x4 -> x0, starting transfers between devices: 28.6 us -> none  [the longest x3 17.4 us: from_everyone(): return lax.all_to_all(copies, axis, split_axis=0, concat_axis=0, tiled=True)]
    broadcast_in_dim x21 -> x0, local copies, waits for them, and re-layouts: 16.9 us -> none  [the longest x10 12.9 us: shards(): jnp.where(take[None, None, :, :, None], small[:, :, :, None, :], sibling[...]
    all_to_all x1 -> x0, blocking collectives: 12.7 us -> none  [sum_at_owner(): lax.all_to_all(parts, axis, split_axis=0, concat_axis=0, tiled=True)]
    dynamic_slice x16 -> x0, local copies, waits for them, and re-layouts: 12.4 us -> none  [the longest x8 7.79 us: one_block(): cols = lax.dynamic_slice_in_dim(bins, index * width, width, 1)]
    eq x9 -> x0, other arithmetic: 12.1 us -> none  [the longest x8 12.1 us: one_block(): cols[:, :, None] == levels[None, None, :]]
    dot_general x8 -> x0, matrix products: 9.93 us -> none  [one_block(): jnp.einsum('rk,rm->km', onehot, spread, preferred_element_type=jnp.float32)]
  transfers between devices with their start and end apart: 4 -> 0, of which waited for: 3 -> 0; matrix products, arithmetic and copies ran while one was open for 8% -> 0% of each run, Pallas kernels for 0% -> 0%
where the time goes in v1:
time: 61.3 us; the launch traced here: 61 us
  Pallas kernels  53.6 us (87%)
  local copies, waits for them, and re-layouts  6.71 us (11%)
  between operations  0.65 us (1%)
    pallas_call x1, Pallas kernels, shards(): pl.pallas_call(kernel, out_shape=(jax.ShapeDtypeStruct((1, 2, 6144), f32)...  53.6 us
    unnamed x15, local copies, waits for them, and re-layouts  6.71 us

profile of v1, /device:TPU:1, one launch (start us, length us, event | category | flops | bytes accessed | tf_op | source)
XLA Modules:
  0.0 61.0 jit_solution(4299884396739997508)
XLA Ops:
  0.6 0.0 copy-start
  0.6 1.6 %copy-done = s32[2048,256]{1,0:T(8,128)S(1)} copy-done((s32[2048,256]{1,0:T(8,128)S(1)}, s32[2048,256]{1,0:T(8,128)}, u32[]{:S(2)}) %copy-start) | copy-done | bytes 2097176
  2.2 0.0 copy-start.1
  2.2 0.7 %copy-done.1 = f32[1,2,3072]{2,1,0:T(2,128)S(1)} copy-done((f32[1,2,3072]{2,1,0:T(2,128)S(1)}, f32[1,2,3072]{2,1,0:T(2,128)}, u32[]{:S(2)}) %copy-start.1) | copy-done | bytes 24600
  3.0 0.0 copy-start.2
  3.0 0.7 %copy-done.2 = s32[1,2048]{1,0:T(1,128)S(1)} copy-done((s32[1,2048]{1,0:T(1,128)S(1)}, s32[1,2048]{1,0:T(1,128)}, u32[]{:S(2)}) %copy-start.2) | copy-done | bytes 8216
  3.7 0.0 copy-start.3
  3.7 0.7 %copy-done.3 = s32[1,2048]{1,0:T(1,128)S(1)} copy-done((s32[1,2048]{1,0:T(1,128)S(1)}, s32[1,2048]{1,0:T(1,128)}, u32[]{:S(2)}) %copy-start.3) | copy-done | bytes 8216
  4.4 0.0 copy-start.4
  4.4 0.7 %copy-done.4 = f32[2048]{0:T(1024)S(1)} copy-done((f32[2048]{0:T(1024)S(1)}, f32[2048]{0:T(1024)}, u32[]{:S(2)}) %copy-start.4) | copy-done | bytes 8216
  5.1 0.0 copy-start.5
  5.1 0.7 %copy-done.5 = s32[1,32]{1,0:T(1,128)S(1)} copy-done((s32[1,32]{1,0:T(1,128)S(1)}, s32[1,32]{1,0:T(1,128)}, u32[]{:S(2)}) %copy-start.5) | copy-done | bytes 152
  5.7 53.6 %shard_map.85 = (f32[1,2,6144]{2,1,0:T(2,128)S(1)}, f32[1,64]{1,0:T(1,128)S(1)}, f32[1,2]{1,0:T(1,128)S(1)}) custom-call(s32[1,2048]{1,0:T(1,128)S(1)} %copy-done.2, s32[1,2048]{1,0:T(1,128)S(1)} %copy-done.3, s32[1,32]{1,0:T(1,128)S(1)} %copy-done.5, s32[2048,256]{1,0:T(8,128)S(1)} %copy-done, f32[1,2048]{1,0:T(1,128)S(1)} %bitcast.2, ...), custom_call_target="tpu_custom_call" | custom-call | tf_op jit(solution)/shard_map/pallas_call | solution.py:374
  59.3 0.6 %copy.12 = f32[1,2,6144]{2,1,0:T(2,128)} copy(f32[1,2,6144]{2,1,0:T(2,128)S(1)} %get-tuple-element.12) | data formatting | bytes 98304
  60.0 0.5 copy.13
  60.5 0.5 copy.14
Async XLA Ops:
  0.6 1.6 %copy-start = (s32[2048,256]{1,0:T(8,128)S(1)}, s32[2048,256]{1,0:T(8,128)}, u32[]{:S(2)}) copy-start(s32[2048,256]{1,0:T(8,128)} %bins_h.1) | copy-start | bytes 6291460
  2.2 0.7 %copy-start.1 = (f32[1,2,3072]{2,1,0:T(2,128)S(1)}, f32[1,2,3072]{2,1,0:T(2,128)}, u32[]{:S(2)}) copy-start(f32[1,2,3072]{2,1,0:T(2,128)} %par_h.1) | copy-start | bytes 73732
  3.0 0.7 %copy-start.2 = (s32[1,2048]{1,0:T(1,128)S(1)}, s32[1,2048]{1,0:T(1,128)}, u32[]{:S(2)}) copy-start(s32[1,2048]{1,0:T(1,128)} %node_h.1) | copy-start | bytes 24580
  3.7 0.7 %copy-start.3 = (s32[1,2048]{1,0:T(1,128)S(1)}, s32[1,2048]{1,0:T(1,128)}, u32[]{:S(2)}) copy-start(s32[1,2048]{1,0:T(1,128)} %bag_h.1) | copy-start | bytes 24580
  4.4 0.7 %copy-start.4 = (f32[2048]{0:T(1024)S(1)}, f32[2048]{0:T(1024)}, u32[]{:S(2)}) copy-start(f32[2048]{0:T(1024)} %param.10) | copy-start | bytes 24580
  5.1 0.7 %copy-start.5 = (s32[1,32]{1,0:T(1,128)S(1)}, s32[1,32]{1,0:T(1,128)}, u32[]{:S(2)}) copy-start(s32[1,32]{1,0:T(1,128)} %flag_h.1) | copy-start | bytes 388

commit v2 on v1

v2 whole, which is shorter than its diff:
```python
import functools

import jax
import jax.numpy as jnp
from jax import lax
from jax.experimental import pallas as pl
from jax.experimental.pallas import tpu as pltpu
from jax.sharding import Mesh
from jax.sharding import PartitionSpec as P

ROWS = ("rows_0", "rows_1", "rows_2")
MESH = pl.DeviceIdType.MESH
HIGHEST = lax.Precision.HIGHEST
f32 = jnp.float32
bf16 = jnp.bfloat16
i32 = jnp.int32

NR = 2048
LOW = -3.0e38


def iota(shape, dim):
    return lax.broadcasted_iota(i32, shape, dim)


def kernel(
    node_h, bag_h, flag_h, bins_h, tgt_h, par_h,
    child_o, best_o, imp_o,
    node_v, bag_v, flag_v, bins_v, tgt_v, par_v,
    bins_b, ev, spread, own, peer, core_r, ring_r, turned, quad_r,
    p16, pchild, amat,
    best_s, best_ra, best_t, best_rb, imp_s, imp_r,
    in_sem, core_ss, core_rs, ring_ss, ring_rs, quad_ss, quad_rs,
    ba_ss, ba_rs, bb_ss, bb_rs, im_ss, im_rs,
):
    z = lax.axis_index("rows_0")
    y = lax.axis_index("rows_1")
    c = lax.axis_index("rows_2")
    t = lax.axis_index("trees")

    def wrap(v, n):
        return jnp.where(v >= n, v - n, v)

    def along_y(off, oc=0):
        return (z, wrap(y + off, 8), 1 - c if oc else c, t)

    def along_z(off):
        return (wrap(z + off, 8), y, c, t)

    def along_x(off):
        return (z, y, c, wrap(t + off, 4))

    def along_p(off):
        return (wrap(z + off * c, 8), wrap(y + off * (1 - c), 8), c, t)

    def along_q(off):
        return (wrap(z + off * (1 - c), 8), wrap(y + off * c, 8), c, t)

    next_p, prev_p = along_p(1), along_p(7)
    qpos = z * (1 - c) + y * c

    small = []
    for i, (src, dst) in enumerate(
        ((node_h, node_v), (bag_h, bag_v), (flag_h, flag_v), (tgt_h, tgt_v), (par_h, par_v))
    ):
        cp = pltpu.make_async_copy(src, dst, in_sem.at[8 + i])
        cp.start()
        small.append(cp)
    loads = []
    for i in range(8):
        cp = pltpu.make_async_copy(
            bins_h.at[pl.ds(256 * i, 256)], bins_v.at[pl.ds(256 * i, 256)], in_sem.at[i]
        )
        cp.start()
        loads.append(cp)

    barrier = pltpu.get_barrier_semaphore()
    greeted = 0
    for oy in range(8):
        for oc in range(2):
            if oy or oc:
                pl.semaphore_signal(barrier, inc=1, device_id=along_y(oy, oc), device_id_type=MESH)
                greeted += 1
    for off in range(1, 8):
        pl.semaphore_signal(barrier, inc=1, device_id=along_z(off), device_id_type=MESH)
        greeted += 1
    for off in range(1, 4):
        pl.semaphore_signal(barrier, inc=1, device_id=along_x(off), device_id_type=MESH)
        greeted += 1

    with jax.named_scope("stats"):
        for cp in small:
            cp.wait()
        flags = flag_v[...]
        row96 = iota((96, 1), 0)
        pair96 = lax.div(row96, 3)
        stat96 = row96 - 3 * pair96
        flag96 = jnp.sum(
            jnp.where(iota((96, 32), 1) == lax.div(iota((96, 32), 0), 3), flags, 0), axis=1, keepdims=True
        )
        chosen = 2 * pair96 + flag96
        for i in range(4):
            part = pl.ds(512 * i, 512)
            node = node_v[:, part]
            wk = bag_v[:, part].astype(f32)
            tgt = tgt_v[:, part]
            first = wk * tgt
            second = first * tgt
            stat = jnp.where(stat96 == 0, wk, jnp.where(stat96 == 1, first, second))
            spread[:, part] = jnp.where(node == chosen, stat, 0.0).astype(bf16)

    with jax.named_scope("cast"):
        for j in range(8):
            loads[j].wait()
            part = pl.ds(256 * j, 256)
            bins_b[part, :] = bins_v[part, :].astype(bf16)

    lane256 = iota((1, 256), 1)
    lane_dd = lax.div(lane256, 128)
    lane_q = lax.rem(lax.div(lane256, 16), 8)
    lane_k = lax.rem(lax.div(lane256, 8), 2)
    lane_b = (4 * lax.rem(lane256, 8)).astype(f32)

    def expander(i, h):
        pos = y * (1 - h) + z * h
        d0 = wrap(pos + 4 + i, 8)
        d1 = wrap(pos + 3 - i, 8)
        d = wrap(d0, 8) * (1 - lane_dd) + d1 * lane_dd
        source = lane_q * (32 - 28 * h) + d * (4 + 28 * h) + 2 * h + lane_k
        return jnp.where(iota((256, 256), 0) == source, 1.0, 0.0).astype(bf16)

    def widen(buf, expand, top):
        for i in (2 * top, 2 * top + 1):
            part = slice(512 * i, 512 * i + 512)
            ev[buf, part, :] = jnp.dot(bins_b[part, :], expand, preferred_element_type=f32).astype(bf16)

    def hot(i, dst, buf, top):
        for bh in (2 * top, 2 * top + 1):
            level = (lane_b + float(bh)).astype(bf16)
            acc = None
            for k in range(8):
                part = slice(256 * k, 256 * k + 256)
                hit = jnp.where(ev[buf, part, :] == level, jnp.ones((), bf16), jnp.zeros((), bf16))
                term = jnp.dot(spread[:, part], hit, preferred_element_type=f32)
                acc = term if acc is None else acc + term
            at = slice(96 * bh, 96 * bh + 96)
            dst[2 * i, at, :] = acc[:, :128]
            dst[2 * i + 1, at, :] = acc[:, 128:]

    def core_copy(i, top):
        part = (pl.ds(2 * i, 2), pl.ds(192 * top, 192))
        return pltpu.make_async_remote_copy(
            src_ref=peer.at[part], dst_ref=core_r.at[part],
            send_sem=core_ss.at[i, top], recv_sem=core_rs.at[i, top],
            device_id=(z, y, 1 - c, t), device_id_type=MESH,
        )

    def merge_core(i, top):
        core_copy(i, top).wait_recv()
        for slot in (2 * i, 2 * i + 1):
            own[slot, 192 * top : 192 * top + 192, :] += core_r[slot, 192 * top : 192 * top + 192, :]

    def ring_copy(way, step, slot, piece):
        rows = pl.ds(96 * piece, 96)
        return pltpu.make_async_remote_copy(
            src_ref=own.at[slot, rows], dst_ref=ring_r.at[way, step, rows],
            send_sem=ring_ss.at[way, step, piece], recv_sem=ring_rs.at[way, step, piece],
            device_id=prev_p if way else next_p, device_id_type=MESH,
        )

    def ring_piece(step, j):
        for way in (0, 1):
            slot = 2 * step if way else 2 * step - 1
            piece = j if way else (j + 2) % 4
            rows = slice(96 * piece, 96 * piece + 96)

            def arrived(way=way, slot=slot, piece=piece, rows=rows):
                ring_copy(way, step - 1, slot, piece).wait_recv()
                own[slot, rows, :] += ring_r[way, step - 1, rows, :]

            if j >= 2:
                arrived()
            else:
                pl.when(step >= 2)(arrived)
            ring_copy(way, step, slot, piece).start()

    widen(0, expander(0, 1 - c), 0)
    widen(0, expander(0, 1 - c), 1)
    with jax.named_scope("barrier_wait"):
        pl.semaphore_wait(barrier, greeted)

    def one_pair(i, carry):
        def ring(j):
            @pl.when(i >= 2)
            def _():
                with jax.named_scope(f"ring{j}"):
                    ring_piece(i - 1, j)

        mine = expander(i, c)
        with jax.named_scope("seg0"):
            widen(1, mine, 0)
            hot(i, peer, 0, 0)
        core_copy(i, 0).start()
        ring(0)
        with jax.named_scope("seg1"):
            widen(1, mine, 1)
            hot(i, peer, 0, 1)
        core_copy(i, 1).start()
        ring(1)
        later = expander(i + 1, 1 - c)
        with jax.named_scope("seg2"):
            widen(0, later, 0)
            hot(i, own, 1, 0)
        with jax.named_scope("merge0"):
            merge_core(i, 0)
        ring(2)
        with jax.named_scope("seg3"):
            widen(0, later, 1)
            hot(i, own, 1, 1)
        with jax.named_scope("merge1"):
            merge_core(i, 1)
        ring(3)

        @pl.when(i == 0)
        def _():
            for piece in (0, 1):
                ring_copy(0, 0, 0, piece).start()
                ring_copy(1, 0, 0, 2 + piece).start()

        return carry

    lax.fori_loop(0, 4, one_pair, 0)
    with jax.named_scope("step3"):
        for j in range(4):
            ring_piece(3, j)

        flag384 = jnp.concatenate([flag96] * 4, axis=0)
        out_lane = iota((1, 768), 1)
        out_bh = lax.div(out_lane, 192)
        out_rest = out_lane - 192 * out_bh
        out_pair = lax.div(out_rest, 6)
        out_six = out_rest - 6 * out_pair
        out_child = lax.div(out_six, 3)
        out_from = 96 * out_bh + 3 * out_pair + (out_six - 3 * out_child)
        for k in range(2):
            for bl in range(8):
                p16[8 * k + bl : 8 * k + bl + 1, :] = par_v[0, k : k + 1, 384 * bl : 384 * bl + 384]
        match = iota((384, 768), 0) == out_from
        is_small = flag384 == out_child
        amat[...] = jnp.where(match, jnp.where(is_small, 1.0, -1.0), 0.0)
        bmat = jnp.where(match, jnp.where(is_small, 0.0, 1.0), 0.0)
        parent = p16[...]
        pchild[...] = jnp.dot(parent, bmat, preferred_element_type=f32, precision=HIGHEST)

    lane = iota((16, 384), 1)
    sub = lax.rem(iota((16, 384), 0), 8)

    def cumulative(x):
        x1 = x + jnp.where(lane >= 96, pltpu.roll(x, 96, 1), 0.0)
        x2 = x1 + jnp.where(lane >= 192, pltpu.roll(x1, 192, 1), 0.0)
        t3 = jnp.where(lane >= 288, x2, 0.0)
        t4 = t3 + pltpu.roll(t3, 96, 1)
        tot = t4 + pltpu.roll(t4, 192, 1)
        before = jnp.where(sub >= 1, pltpu.roll(tot, 1, 0), 0.0)
        for s in (1, 2, 4):
            before = before + jnp.where(sub >= s, pltpu.roll(before, s, 0), 0.0)
        whole = jnp.sum(tot.reshape(2, 8, 384), axis=1, keepdims=True)
        whole = jnp.broadcast_to(whole, (2, 8, 384)).reshape(16, 384)
        return x2 + before, whole

    def gain_of(cb, sb, call, sall):
        gain = sb * sb / (jnp.maximum(cb, 0.0) + 1.0)
        rest = sall - sb
        gain = gain + rest * rest / (jnp.maximum(call - cb, 0.0) + 1.0)
        gain = gain - sall * sall / (jnp.maximum(call, 0.0) + 1.0)
        gain = jnp.where((sub == 7) & (lane >= 288), LOW, gain)
        top = jnp.max(gain.reshape(2, 8, 384), axis=1, keepdims=True)
        top = jnp.broadcast_to(top, (2, 8, 384)).reshape(16, 384)
        top = jnp.maximum(top, pltpu.roll(top, 192, 1))
        return jnp.maximum(top, pltpu.roll(top, 96, 1))

    def left_one(x):
        return pltpu.roll(x, 383, 1)

    with jax.named_scope("parents2"):
        pcum, pall = cumulative(parent)
        psum, psall = left_one(pcum), left_one(pall)

    with jax.named_scope("ring_end"):
        for piece in range(4):
            for way in (0, 1):
                ring_copy(way, 3, 0, piece).wait_recv()
    with jax.named_scope("turn"):
        total = own[7] + ring_r[0, 3] + ring_r[1, 3]
        turned[...] = total.T

    def quad_copy(off):
        to = wrap(qpos + off, 8)
        return pltpu.make_async_remote_copy(
            src_ref=turned.at[pl.ds(pl.multiple_of(16 * to, 16), 16)], dst_ref=quad_r.at[off],
            send_sem=quad_ss.at[off], recv_sem=quad_rs.at[off],
            device_id=along_q(off), device_id_type=MESH,
        )

    far_first = (4, 3, 5, 2, 6, 1, 7)
    for off in far_first:
        quad_copy(off).start()
    with jax.named_scope("quad"):
        hist = turned[pl.ds(pl.multiple_of(16 * qpos, 16), 16), :]
        for off in (1, 7, 2, 6, 3, 5, 4):
            quad_copy(off).wait_recv()
            hist = hist + quad_r[off]

    with jax.named_scope("gains"):
        scum, sall = cumulative(hist)
        ssum, ssall = left_one(scum), left_one(sall)
        gain_s = gain_of(scum, ssum, sall, ssall)
        gain_b = gain_of(pcum - scum, psum - ssum, pall - sall, psall - ssall)
        third = lax.rem(lane, 3)
        both = jnp.where((lane < 96) & (third == 0), gain_s + gain_b, 0.0)
        feat = jnp.sum(both, axis=1, keepdims=True)
        lane8 = iota((8, 128), 1)
        imp_s[...] = jnp.where(lane8 == 0, feat[0:8], jnp.where(lane8 == 1, feat[8:16], 0.0))
        top_s = jnp.maximum(gain_s[0:8], gain_s[8:16])
        top_b = jnp.maximum(gain_b[0:8], gain_b[8:16])
        mixed = jnp.where(third[0:8] == 0, top_s, pltpu.roll(top_b, 1, 1))
        best_s[...] = mixed[:, :128]

    def best_a(oy, oc):
        slot = 2 * oy + oc
        return pltpu.make_async_remote_copy(
            src_ref=best_s, dst_ref=best_ra.at[slot],
            send_sem=ba_ss.at[slot], recv_sem=ba_rs.at[slot],
            device_id=along_y(oy, oc), device_id_type=MESH,
        )

    def best_b(off):
        return pltpu.make_async_remote_copy(
            src_ref=best_t, dst_ref=best_rb.at[off],
            send_sem=bb_ss.at[off], recv_sem=bb_rs.at[off],
            device_id=along_z(off), device_id_type=MESH,
        )

    def imp_copy(off):
        return pltpu.make_async_remote_copy(
            src_ref=imp_s, dst_ref=imp_r.at[off],
            send_sem=im_ss.at[off], recv_sem=im_rs.at[off],
            device_id=along_x(off), device_id_type=MESH,
        )

    others = [(oy, oc) for oy in (4, 3, 5, 2, 6, 1, 7, 0) for oc in (0, 1) if oy or oc]
    for oy, oc in others:
        best_a(oy, oc).start()
    for off in (2, 1, 3):
        imp_copy(off).start()

    with jax.named_scope("kids"):
        kids = pchild[...] + jnp.dot(hist, amat[...], preferred_element_type=f32, precision=HIGHEST)
        for k in range(2):
            for bl in range(8):
                child_o[0, k : k + 1, 768 * bl : 768 * bl + 768] = kids[8 * k + bl : 8 * k + bl + 1, :]

    with jax.named_scope("best_a"):
        top = best_s[...]
        for oy, oc in others:
            best_a(oy, oc).wait_recv()
            top = jnp.maximum(top, best_ra[2 * oy + oc])
    best_t[...] = top
    for off in far_first:
        best_b(off).start()

    with jax.named_scope("pick"):
        flag_col = jnp.sum(jnp.where(iota((32, 32), 0) == iota((32, 32), 1), flags, 0), axis=1, keepdims=True)
        node_lane = iota((32, 64), 1)
        node_flag = jnp.sum(
            jnp.where(lax.div(node_lane, 2) == iota((32, 64), 0), flag_col, 0), axis=0, keepdims=True
        )
        q_lane = iota((1, 64), 1)
        q_pair = lax.div(q_lane, 2)
        taken = 3 * q_pair + jnp.where(q_lane - 2 * q_pair == node_flag, 0, 1)
        pick = jnp.where(iota((128, 64), 0) == taken, 1.0, 0.0)

    with jax.named_scope("imp"):
        share = imp_s[...]
        for off in (1, 3, 2):
            imp_copy(off).wait_recv()
            share = share + imp_r[off]
        imp_o[...] = share[0:1, 0:2] * (1.0 / 256.0)

    with jax.named_scope("best_b"):
        for off in far_first:
            best_b(off).wait_recv()
            top = jnp.maximum(top, best_rb[off])
    best_o[...] = jnp.dot(top, pick, preferred_element_type=f32, precision=HIGHEST)[0:1, :]

    with jax.named_scope("sends"):
        for i in range(4):
            for top in (0, 1):
                core_copy(i, top).wait_send()
        for way in (0, 1):
            for step in range(4):
                for piece in range(4) if step else (2 * way, 2 * way + 1):
                    ring_copy(way, step, 0, piece).wait_send()
        for off in range(1, 8):
            quad_copy(off).wait_send()
            best_b(off).wait_send()
        for oy, oc in others:
            best_a(oy, oc).wait_send()
        for off in range(1, 4):
            imp_copy(off).wait_send()


def hand_over(child, best, imp, child_o, best_o, imp_o):
    child_o[...] = child[...]
    best_o[...] = best[...]
    imp_o[...] = imp[...]


def shards(node_of_row, bag_weight, smaller_side, bins, target, parent_hist):
    any_space = pl.BlockSpec(memory_space=pltpu.HBM)
    vmem = pl.BlockSpec(memory_space=pltpu.VMEM)
    dma = pltpu.SemaphoreType.DMA
    shapes = (
        jax.ShapeDtypeStruct((1, 2, 6144), f32),
        jax.ShapeDtypeStruct((1, 64), f32),
        jax.ShapeDtypeStruct((1, 2), f32),
    )
    results = pl.pallas_call(
        kernel,
        out_shape=shapes,
        in_specs=[any_space] * 6,
        out_specs=(vmem, vmem, vmem),
        scratch_shapes=[
            pltpu.VMEM((1, NR), i32),
            pltpu.VMEM((1, NR), i32),
            pltpu.VMEM((1, 32), i32),
            pltpu.VMEM((NR, 256), i32),
            pltpu.VMEM((1, NR), f32),
            pltpu.VMEM((1, 2, 3072), f32),
            pltpu.VMEM((NR, 256), bf16),
            pltpu.VMEM((2, NR, 256), bf16),
            pltpu.VMEM((96, NR), bf16),
            pltpu.VMEM((8, 384, 128), f32),
            pltpu.VMEM((8, 384, 128), f32),
            pltpu.VMEM((8, 384, 128), f32),
            pltpu.VMEM((2, 4, 384, 128), f32),
            pltpu.VMEM((128, 384), f32),
            pltpu.VMEM((8, 16, 384), f32),
            pltpu.VMEM((16, 384), f32),
            pltpu.VMEM((16, 768), f32),
            pltpu.VMEM((384, 768), f32),
            pltpu.VMEM((8, 128), f32),
            pltpu.VMEM((16, 8, 128), f32),
            pltpu.VMEM((8, 128), f32),
            pltpu.VMEM((8, 8, 128), f32),
            pltpu.VMEM((8, 128), f32),
            pltpu.VMEM((4, 8, 128), f32),
            dma((13,)),
            dma((4, 2)), dma((4, 2)),
            dma((2, 4, 4)), dma((2, 4, 4)),
            dma((8,)), dma((8,)),
            dma((16,)), dma((16,)),
            dma((8,)), dma((8,)),
            dma((4,)), dma((4,)),
        ],
        compiler_params=pltpu.CompilerParams(
            collective_id=0, has_side_effects=True, vmem_limit_bytes=67_043_328
        ),
    )(node_of_row, bag_weight, smaller_side, bins, target.reshape(1, NR), parent_hist)
    child, best, imp = pl.pallas_call(
        hand_over, out_shape=shapes, in_specs=[vmem] * 3, out_specs=(vmem, vmem, vmem)
    )(*results)
    return child, best, imp.reshape(2)


def solution(mesh):
    finer = Mesh(
        mesh.devices.reshape(8, 8, 2, mesh.shape["trees"]), ("rows_0", "rows_1", "rows_2", "trees")
    )
    return jax.shard_map(
        shards,
        mesh=finer,
        in_specs=(
            P("trees", ROWS),
            P("trees", ROWS),
            P("trees", None),
            P(ROWS, None),
            P(ROWS),
            P("trees", ROWS, None),
        ),
        out_specs=(P("trees", ROWS, None), P("trees", None), P(ROWS)),
        check_vma=False,
    )
```

time: 61.3 us -> 52.3 us (0.85)
  local copies, waits for them, and re-layouts: 6.71 us -> 0 us
  Pallas kernels: 53.6 us -> 51.4 us
    unnamed x15 -> x0, local copies, waits for them, and re-layouts: 6.71 us -> none
    pallas_call x1 -> x2, Pallas kernels: 53.6 us -> 51.4 us  [the longest x1 50 us: shards(): pl.pallas_call(kernel, out_shape=shapes, in_specs=[any_space] * 6, out_sp...]
where the time goes in v2:
time: 52.3 us; the launch traced here: 52.1 us
  Pallas kernels  51.4 us (98%)
  between operations  0.64 us (1%)
    pallas_call x1, Pallas kernels, shards(): pl.pallas_call(kernel, out_shape=shapes, in_specs=[any_space] * 6, out_sp...  50 us
    pallas_call x1, Pallas kernels, shards(): pl.pallas_call(hand_over, out_shape=shapes, in_specs=[vmem] * 3, out_spec...  1.43 us

profile of v2, /device:TPU:1, one launch (start us, length us, event | category | flops | bytes accessed | tf_op | source)
XLA Modules:
  0.0 52.1 jit_solution(231596604863212664)
XLA Ops:
  0.6 50.0 %shard_map.85 = (f32[1,2,6144]{2,1,0:T(2,128)}, f32[1,64]{1,0:T(1,128)}, f32[1,2]{1,0:T(1,128)}) custom-call(s32[1,2048]{1,0:T(1,128)} %node_h.1, s32[1,2048]{1,0:T(1,128)} %bag_h.1, s32[1,32]{1,0:T(1,128)} %flag_h.1, s32[2048,256]{1,0:T(8,128)} %bins_h.1, f32[1,2048]{1,0:T(1,128)} %bitcast.2, f32[1,2,3072]{2,1,0:T(2,128)} %par_h.1), custom_call_target="tpu_custom_call" | custom-call | tf_op jit(solution)/shard_map/pallas_call | solution.py:428
  50.6 1.4 %shard_map.86 = (f32[1,2,6144]{2,1,0:T(2,128)}, f32[1,64]{1,0:T(1,128)}, f32[1,2]{1,0:T(1,128)}) custom-call(f32[1,2,6144]{2,1,0:T(2,128)} %get-tuple-element.9.child, f32[1,64]{1,0:T(1,128)} %get-tuple-element.10.best, f32[1,2]{1,0:T(1,128)} %get-tuple-element.11.imp), custom_call_target="tpu_custom_call" | custom-call | tf_op jit(solution)/shard_map/pallas_call | solution.py:470
